TPU v7x, 32 devices: a whole 2x2x4 slice. The times are simulated.
32 devices in a mesh: row: 4 (over x, core), col: 8 (over z, y).
Axes of the slice: x: 2, y: 2, z: 4, core: 2. Of those that a mesh axis runs over, the one named last changes fastest.
Arguments:
- rows: bfloat16 [1024, 4096], P(('row', 'col')), may hold values from -6 to 6
- task_ids: int32 [1024], P(('row', 'col')), may hold values from 0 to 8, as said below
- task_embed: bfloat16 [8, 4096], replicated, may hold values from -6 to 6
- norm_gain: float32 [4, 4096], replicated, may hold values from 0.1 to 1.9
- layer_weight: bfloat16 [4, 4096, 4096], P(None, None, 'col'), may hold values from -0.09375 to 0.09375
Outputs:
- packed_out: bfloat16 [1024, 4096], P('row', 'col')
Inputs may be any that keep to these rules, and one draw needn't show every extreme that they name: `task_ids`: 8 marks an empty row, smaller values name a task.
All inputs are finite; a program needn't handle non-finite values.
Results may differ from a plain program's by a relative error of at most 0.008.
Values may be sent and summed in bfloat16 or wider, within the bound.
A program may use at most 128 MiB of HBM per device.

v0:
```python
import functools

import jax
import jax.numpy as jnp
from jax import lax
from jax.experimental import pallas as pl
from jax.experimental.pallas import tpu as pltpu
from jax.sharding import PartitionSpec as P

epsilon = 1e-06
MESH = pl.DeviceIdType.MESH
INNER = 2
CHUNKS = 4
LEAD1 = 2
LEAD2 = 1
F32 = jnp.float32
BF16 = jnp.bfloat16


def kernel(
    sizes,
    rows_ref,
    ids_ref,
    embed_ref,
    gain_ref,
    weight_ref,
    out_ref,
    weight,
    hidden,
    active,
    gain,
    pieces,
    outgo,
    income,
    id_own,
    id_row,
    id_sum,
    id_col,
    sem_weight,
    send_piece,
    recv_piece,
    send_idrow,
    recv_idrow,
    send_idcol,
    recv_idcol,
    send_row,
    recv_row,
    send_own,
    send_relay,
    send_along,
    recv_hidden,
):
    n_row, n_col, layers, chunks, tasks, cap = sizes
    n_outer = n_col // INNER
    rows_dev = rows_ref.shape[0]
    width = rows_ref.shape[1]
    part = width // n_col
    slots = rows_dev * n_col
    m = slots // chunks
    steps = layers * chunks
    me_r = lax.axis_index("row")
    me_c = lax.axis_index("col")
    outer = me_c // INNER
    inner = me_c % INNER
    partner = outer * INNER + (INNER - 1 - inner)

    def col_peer(j):
        return (me_c + j) % n_col

    def row_peer(j):
        return (me_r + j) % n_row

    def outer_peer(j):
        return ((outer + j) % n_outer) * INNER + inner

    def remote(src, dst, send, recv, r, c):
        return pltpu.make_async_remote_copy(
            src_ref=src, dst_ref=dst, send_sem=send, recv_sem=recv, device_id=(r, c), device_id_type=MESH
        )

    def weight_copy(l):
        return pltpu.make_async_copy(weight_ref.at[l], weight.at[l], sem_weight.at[l])

    lead_dim = id_own.shape[0]
    spread = lax.broadcasted_iota(jnp.int32, (rows_dev, slots), 1) - lax.broadcasted_iota(
        jnp.int32, (rows_dev, slots), 0
    )
    spread = jnp.where(spread == me_c * rows_dev, 1.0, 0.0).astype(BF16)
    own_ids = jnp.broadcast_to(ids_ref[...].astype(F32), (lead_dim, rows_dev)).astype(BF16)
    own_ids = jnp.dot(own_ids, spread, preferred_element_type=F32).astype(jnp.int32)
    sub = lax.broadcasted_iota(jnp.int32, (lead_dim, slots), 0)
    id_own[...] = jnp.where(sub == me_r, own_ids, 0)

    barrier = pltpu.get_barrier_semaphore()
    for j in range(1, n_row):
        pl.semaphore_signal(barrier, inc=1, device_id=(row_peer(j), me_c), device_id_type=MESH)
    for j in range(1, n_col):
        pl.semaphore_signal(barrier, inc=1, device_id=(me_r, col_peer(j)), device_id_type=MESH)
    pl.semaphore_wait(barrier, n_row + n_col - 2)

    def id_row_copy(j):
        return remote(id_own, id_row.at[me_r], send_idrow.at[j], recv_idrow.at[me_r], row_peer(j), me_c)

    def id_row_from(j):
        return remote(id_own, id_row.at[row_peer(j)], send_idrow.at[j], recv_idrow.at[row_peer(j)], row_peer(j), me_c)

    def columns(c):
        return pl.ds(pl.multiple_of(c * part, part), part)

    def piece_copy(j):
        return remote(
            rows_ref.at[:, columns(col_peer(j))], pieces.at[me_c], send_piece.at[j], recv_piece.at[me_c], me_r, col_peer(j)
        )

    def piece_from(j):
        return remote(
            rows_ref.at[:, columns(col_peer(j))], pieces.at[col_peer(j)], send_piece.at[j], recv_piece.at[col_peer(j)],
            me_r, col_peer(j),
        )

    for j in range(1, n_row):
        id_row_copy(j).start()
    for j in range(1, n_col):
        piece_copy(j).start()
    for l in range(layers):
        weight_copy(l).start()
    pieces[me_c] = rows_ref[:, columns(me_c)]
    for l in range(layers):
        gain[l] = gain_ref[l : l + 1, :]

    ids_here = id_own[...]
    for j in range(1, n_row):
        id_row_from(j).wait_recv()
        ids_here = ids_here + id_row[row_peer(j)]
    id_sum[...] = ids_here

    def id_col_copy(j):
        return remote(id_sum, id_col.at[me_c], send_idcol.at[j], recv_idcol.at[me_c], me_r, col_peer(j))

    def id_col_from(j):
        return remote(id_sum, id_col.at[col_peer(j)], send_idcol.at[j], recv_idcol.at[col_peer(j)], me_r, col_peer(j))

    for j in range(1, n_col):
        id_col_copy(j).start()
    low = lax.broadcasted_iota(jnp.int32, (slots, slots), 0)
    high = lax.broadcasted_iota(jnp.int32, (slots, slots), 1)
    earlier = jnp.where(low < high, 1.0, 0.0).astype(BF16)
    ids = ids_here
    for j in range(1, n_col):
        id_col_from(j).wait_recv()
        ids = ids + id_col[col_peer(j)]

    sub_col = lax.broadcasted_iota(jnp.int32, (lead_dim, 1), 0)
    ids = jnp.where(sub < n_row, ids, tasks)
    live = ids < tasks
    member = [jnp.where(ids == t, 1.0, 0.0) for t in range(tasks)]
    ranks = jnp.dot(jnp.concatenate(member, 0).astype(BF16), earlier, preferred_element_type=F32)
    base = jnp.zeros((1, 1), F32)
    bases, ends = [], []
    position = jnp.zeros((lead_dim, slots), F32)
    for t in range(tasks):
        count = jnp.sum(member[t], axis=1, keepdims=True)
        bases.append(base)
        offset = jnp.zeros((lead_dim, 1), F32) + base
        for r in range(n_row):
            here = count[r : r + 1, :]
            offset = offset + jnp.where(sub_col > r, here, 0.0)
            base = base + here
        ends.append(base)
        rank = ranks[t * lead_dim : (t + 1) * lead_dim, :]
        position = position + member[t] * (offset + rank)
    slot = jnp.floor((position + 0.5) * (1.0 / n_row))
    target = jnp.where(live, position - slot * n_row, -1.0)
    aimed = [jnp.where(target == float(r), 1.0, 0.0) for r in range(n_row)]
    places = jnp.dot(jnp.concatenate(aimed, 0).astype(BF16), earlier, preferred_element_type=F32)
    place = jnp.zeros((lead_dim, slots), F32)
    for r in range(n_row):
        place = place + aimed[r] * places[r * lead_dim : (r + 1) * lead_dim, :]
    slot = slot.astype(jnp.int32)
    target = target.astype(jnp.int32)
    place = place.astype(jnp.int32)

    def of_me(values):
        picked = values[0:1, :]
        for r in range(1, n_row):
            picked = jnp.where(me_r == r, values[r : r + 1, :], picked)
        return picked

    cap_range = lax.broadcasted_iota(jnp.int32, (cap, slots), 0)

    def select(target_row, place_row, r):
        return jnp.where((cap_range == place_row) & (target_row == r), 1.0, 0.0).astype(BF16)

    my_target, my_place = of_me(target), of_me(place)
    picks = [select(my_target, my_place, row_peer(j)) for j in range(n_row)]
    slot_range = lax.broadcasted_iota(jnp.int32, (slots, slots), 0)

    for j in range(1, n_col):
        piece_from(j).wait_recv()
    group = pieces[...].reshape(slots, part)

    def row_copy(j):
        return remote(outgo.at[j], income.at[me_r], send_row.at[j], recv_row.at[me_r], row_peer(j), me_c)

    def row_from(j):
        return remote(outgo.at[j], income.at[row_peer(j)], send_row.at[j], recv_row.at[row_peer(j)], row_peer(j), me_c)

    for j in range(1, n_row):
        outgo[j] = jnp.dot(picks[j], group, preferred_element_type=F32).astype(BF16)
        row_copy(j).start()
    income[me_r] = jnp.dot(picks[0], group, preferred_element_type=F32).astype(BF16)

    puts = []
    for r in range(n_row):
        target_row = target[r : r + 1, :]
        here = jnp.where((slot_range == slot[r : r + 1, :]) & (target_row == me_r), 1.0, 0.0).astype(BF16)
        pick = select(target_row, place[r : r + 1, :], me_r)
        puts.append(
            lax.dot_general(here, pick, (((1,), (1,)), ((), ())), preferred_element_type=F32).astype(BF16)
        )
    slot_pos = (lax.broadcasted_iota(jnp.int32, (slots, 1), 0) * n_row + me_r).astype(F32)
    own_embed = embed_ref[:, columns(me_c)].astype(F32)
    start = jnp.zeros((slots, part), F32)
    for t in range(tasks):
        inside = jnp.where((slot_pos >= bases[t]) & (slot_pos < ends[t]), 1.0, 0.0)
        start = start + inside * own_embed[t : t + 1, :]
    for j in range(1, n_row):
        row_from(j).wait_recv()

    half = n_outer // 2
    side = outer // half
    is_gate = outer == half - 1 + side
    far_gate = (half - side) * INNER + inner

    def near(j, i):
        return (side * half + (outer % half + j) % half) * INNER + i

    def far(k, i):
        return ((1 - side) * half + k) * INNER + i

    other = INNER - 1 - inner

    def block_copy(s, source, send, peer):
        block = hidden.at[s, source]
        return remote(block, block, send, recv_hidden.at[s, source], me_r, peer)

    def await_block(s, source):
        block_copy(s, source, send_relay.at[0, source], partner).wait_recv()

    def own_copies(s):
        peers = [near(j, inner) for j in range(1, half)] + [far_gate, partner]
        return [block_copy(s, me_c, send_own.at[s % chunks, peer], peer) for peer in peers]

    def send_all(s):
        for copy in own_copies(s):
            copy.start()

    def drain_own(s):
        for copy in own_copies(s):
            copy.wait_send()

    def over(s, source):
        return block_copy(s, source, send_relay.at[s % chunks, source], partner)

    def along(s, source, j):
        return block_copy(s, source, send_along.at[s % chunks, source // INNER, j], near(j, inner))

    def pass_on(s, go, source, copies):
        if go:
            await_block(s, source)
        for copy in copies:
            if go:
                copy.start()
            else:
                copy.wait_send()

    def first_relay(s, go):
        @pl.when(is_gate)
        def _():
            for k in range(half):
                source = far(k, inner)
                pass_on(s, go, source, [along(s, source, j) for j in range(1, half)] + [over(s, source)])

        @pl.when(s % 2 == 0)
        def _():
            for j in range(1, half):
                pass_on(s, go, near(j, inner), [over(s, near(j, inner))])

        @pl.when(s % 2 == 1)
        def _():
            pass_on(s, go, partner, [along(s, partner, j) for j in range(1, half)])

    def second_relay(s, go):
        @pl.when(jnp.logical_not(is_gate))
        def _():
            for k in range(half):
                pass_on(s, go, far(k, inner), [over(s, far(k, inner))])

    def await_rest(s):
        @pl.when(s % 2 == 0)
        def _():
            await_block(s, partner)

        @pl.when(s % 2 == 1)
        def _():
            for j in range(1, half):
                await_block(s, near(j, inner))

        for j in range(1, half):
            await_block(s, near(j, other))
        for k in range(half):
            await_block(s, far(k, other))

    def relay(s, relay_of):
        @pl.when(s < steps)
        def _():
            @pl.when(s >= chunks)
            def _():
                relay_of(s - chunks, False)

            relay_of(s, True)

    for ch in range(chunks):
        span = slice(ch * m, (ch + 1) * m)
        placed = jnp.zeros((m, part), F32)
        for r in range(n_row):
            placed = placed + jnp.dot(puts[r][span, :], income[r], preferred_element_type=F32)
        hidden[ch, me_c] = (placed + start[span, :]).astype(BF16)
        send_all(ch)
    for s in range(LEAD1):
        first_relay(jnp.int32(s), True)
    for s in range(LEAD2):
        second_relay(jnp.int32(s), True)

    def step(s, carry):
        l = s // chunks
        ch = s % chunks
        relay(s + LEAD2, second_relay)
        relay(s + LEAD1, first_relay)

        @pl.when(ch == 0)
        def _():
            weight_copy(l).wait()

        await_rest(s)
        total = jnp.zeros((m, part), F32)
        for c in range(n_col):
            values = hidden[s, c].astype(F32)
            total = total + values * values
        mean = jnp.sum(total, axis=1, keepdims=True) * (1.0 / width)
        inverse = lax.rsqrt(mean + epsilon)
        for c in range(n_col):
            cols = slice(c * part, (c + 1) * part)
            values = hidden[s, c].astype(F32) * inverse * gain[l, :, cols]
            half = 0.5 * values
            active[:, cols] = (half + half * jnp.tanh(half)).astype(BF16)
        update = jnp.dot(active[...], weight[l], preferred_element_type=F32)
        result = (hidden[s, me_c].astype(F32) + update).astype(BF16)

        drain_own(s)

        @pl.when(l < layers - 1)
        def _():
            hidden[s + chunks, me_c] = result
            send_all(s + chunks)

        @pl.when(l == layers - 1)
        def _():
            out_ref[ch] = result

        return carry

    lax.fori_loop(0, steps, step, 0)

    for ch in range(chunks):
        first_relay(jnp.int32(steps - chunks + ch), False)
        second_relay(jnp.int32(steps - chunks + ch), False)
    for j in range(1, n_row):
        id_row_copy(j).wait_send()
        row_copy(j).wait_send()
    for j in range(1, n_col):
        piece_copy(j).wait_send()
        id_col_copy(j).wait_send()


def shards(rows, task_ids, task_embed, norm_gain, layer_weight):
    rows_dev, width = rows.shape
    tasks = task_embed.shape[0]
    layers = layer_weight.shape[0]
    part = layer_weight.shape[2]
    n_row = lax.axis_size("row")
    n_col = lax.axis_size("col")
    slots = rows_dev * n_col
    cap = -(-(slots // n_row + tasks) // 16) * 16
    chunks = CHUNKS
    m = slots // chunks
    lead_dim = -(-n_row // 8) * 8
    sizes = (n_row, n_col, layers, chunks, tasks, cap)
    dma = pltpu.SemaphoreType.DMA
    vmem = pl.BlockSpec(memory_space=pltpu.VMEM)
    out = pl.pallas_call(
        functools.partial(kernel, sizes),
        out_shape=jax.ShapeDtypeStruct((chunks, m, part), BF16),
        in_specs=[vmem, vmem, vmem, vmem, pl.BlockSpec(memory_space=pl.ANY)],
        out_specs=vmem,
        scratch_shapes=[
            pltpu.VMEM((layers, width, part), BF16),
            pltpu.VMEM((layers * chunks, n_col, m, part), BF16),
            pltpu.VMEM((m, width), BF16),
            pltpu.VMEM((layers, 1, width), F32),
            pltpu.VMEM((n_col, rows_dev, part), BF16),
            pltpu.VMEM((n_row, cap, part), BF16),
            pltpu.VMEM((n_row, cap, part), BF16),
            pltpu.VMEM((lead_dim, slots), jnp.int32),
            pltpu.VMEM((n_row, lead_dim, slots), jnp.int32),
            pltpu.VMEM((lead_dim, slots), jnp.int32),
            pltpu.VMEM((n_col, lead_dim, slots), jnp.int32),
            dma((layers,)),
            dma((n_col,)),
            dma((n_col,)),
            dma((n_row,)),
            dma((n_row,)),
            dma((n_col,)),
            dma((n_col,)),
            dma((n_row,)),
            dma((n_row,)),
            dma((chunks, n_col)),
            dma((chunks, n_col)),
            dma((chunks, n_col // INNER, max(1, n_col // INNER // 2))),
            dma((layers * chunks, n_col)),
        ],
        compiler_params=pltpu.CompilerParams(
            collective_id=0, has_side_effects=True, vmem_limit_bytes=60 * 1024 * 1024
        ),
    )(rows, task_ids.reshape(1, rows_dev), task_embed, norm_gain, layer_weight)
    return out.reshape(slots, part)


def solution(mesh):
    return jax.shard_map(
        shards,
        mesh=mesh,
        in_specs=(P(("row", "col"), None), P(("row", "col")), P(), P(), P(None, None, "col")),
        out_specs=P("row", "col"),
        check_vma=False,
    )
```

profile of v0, /device:TPU:1, one launch (start us, length us, event | category | flops | bytes accessed | tf_op | source)
XLA Modules:
  0.0 108.8 jit_solution(5842373773715598019)
XLA Ops:
  0.0 107.1 %shard_map.55 = bf16[4,64,512]{2,1,0:T(8,128)(2,1)} custom-call(bf16[32,4096]{1,0:T(8,128)(2,1)} %rows_ref.1, s32[1,32]{1,0:T(1,128)} %bitcast.3, bf16[8,4096]{1,0:T(8,128)(2,1)} %embed_ref.1, f32[4,4096]{1,0:T(4,128)} %gain_ref.1, bf16[4,4096,512]{2,1,0:T(8,128)(2,1)} %weight_ref.1), custom_call_target="tpu_custom_call" | custom-call | tf_op jit(solution)/shard_map/pallas_call | solution.py:401
  107.1 1.7 %copy.7 = bf16[256,512]{1,0:T(8,128)(2,1)} copy(bf16[256,512]{1,0:T(8,128)(2,1)} %bitcast.2) | data formatting | bytes 524288
where the time goes:
time: 110 us; the launch traced here: 109 us
  Pallas kernels  107 us (97%)
  local copies, waits for them, and re-layouts  1.67 us (2%)
    pallas_call x1, Pallas kernels, shards(): pl.pallas_call(functools.partial(kernel, sizes), out_shape=jax.ShapeDtype...  107 us

commit v1 on v0

v1 whole, which is shorter than its diff:
```python
import functools

import jax
import jax.numpy as jnp
from jax import lax
from jax.experimental import pallas as pl
from jax.experimental.pallas import tpu as pltpu
from jax.sharding import PartitionSpec as P

epsilon = 1e-06
MESH = pl.DeviceIdType.MESH
INNER = 2
CHUNKS = 4
SUB = 16
LEAD1 = 2
LEAD2 = 1
F32 = jnp.float32
BF16 = jnp.bfloat16


def kernel(
    sizes,
    rows_ref,
    ids_ref,
    embed_ref,
    gain_ref,
    weight_ref,
    out_ref,
    weight,
    hidden,
    active,
    gain,
    income,
    put,
    id_own,
    id_row,
    id_sum,
    id_col,
    sem_weight,
    send_idrow,
    recv_idrow,
    send_idcol,
    recv_idcol,
    send_row,
    recv_row,
    send_own,
    send_relay,
    send_along,
    recv_hidden,
):
    n_row, n_col, layers, chunks, tasks = sizes
    n_outer = n_col // INNER
    rows_dev = rows_ref.shape[0]
    width = rows_ref.shape[1]
    part = width // n_col
    slots = rows_dev * n_col
    m = slots // chunks
    steps = layers * chunks
    groups = rows_dev // SUB
    halves = chunks // groups
    span = n_col // halves
    me_r = lax.axis_index("row")
    me_c = lax.axis_index("col")
    outer = me_c // INNER
    inner = me_c % INNER
    partner = outer * INNER + (INNER - 1 - inner)

    def col_peer(j):
        return (me_c + j) % n_col

    def row_peer(j):
        return (me_r + j) % n_row

    def remote(src, dst, send, recv, r, c):
        return pltpu.make_async_remote_copy(
            src_ref=src, dst_ref=dst, send_sem=send, recv_sem=recv, device_id=(r, c), device_id_type=MESH
        )

    def weight_copy(l):
        return pltpu.make_async_copy(weight_ref.at[l], weight.at[l], sem_weight.at[l])

    barrier = pltpu.get_barrier_semaphore()
    for j in range(1, n_row):
        pl.semaphore_signal(barrier, inc=1, device_id=(row_peer(j), me_c), device_id_type=MESH)
    for j in range(1, n_col):
        pl.semaphore_signal(barrier, inc=1, device_id=(me_r, col_peer(j)), device_id_type=MESH)

    for l in range(layers):
        weight_copy(l).start()

    lead_dim = id_own.shape[0]
    lanes = id_own.shape[1]
    per_tile = lanes // rows_dev
    raw_ids = ids_ref[...]
    spread = lax.broadcasted_iota(jnp.int32, (rows_dev, lanes), 1) - lax.broadcasted_iota(
        jnp.int32, (rows_dev, lanes), 0
    )
    spread = jnp.where(spread == (me_c % per_tile) * rows_dev, 1.0, 0.0).astype(BF16)
    own_ids = jnp.broadcast_to(raw_ids.astype(F32), (lead_dim, rows_dev)).astype(BF16)
    row_ids = jnp.dot(own_ids, spread, preferred_element_type=F32).astype(jnp.int32)
    sub = lax.broadcasted_iota(jnp.int32, (lead_dim, lanes), 0)
    id_own[...] = jnp.where(sub == me_r, row_ids, 0)

    eye = jnp.where(
        lax.broadcasted_iota(jnp.int32, (rows_dev, rows_dev), 0)
        == lax.broadcasted_iota(jnp.int32, (rows_dev, rows_dev), 1),
        1.0,
        0.0,
    ).astype(BF16)
    tall_ids = lax.dot_general(eye, own_ids, (((1,), (1,)), ((), ())), preferred_element_type=F32)[:, 0:1]
    embed_on = [jnp.where(tall_ids == float(t), 1.0, 0.0) for t in range(tasks)]
    for g in range(groups):
        lines = slice(g * SUB, (g + 1) * SUB)
        for c in range(n_col):
            cols = slice(c * part, (c + 1) * part)
            term = jnp.zeros((SUB, part), F32)
            for t in range(tasks):
                term = term + embed_on[t][lines, :] * embed_ref[t : t + 1, cols].astype(F32)
            begin = (rows_ref[lines, cols].astype(F32) + term).astype(BF16)
            hidden[g * halves + c // span, me_c, (c % span) * SUB : (c % span + 1) * SUB, :] = begin

    pl.semaphore_wait(barrier, n_row + n_col - 2)

    def id_row_copy(j):
        return remote(id_own, id_row.at[me_r], send_idrow.at[j], recv_idrow.at[me_r], row_peer(j), me_c)

    def id_row_from(j):
        return remote(id_own, id_row.at[row_peer(j)], send_idrow.at[j], recv_idrow.at[row_peer(j)], row_peer(j), me_c)

    def id_col_copy(j):
        return remote(id_sum, id_col.at[me_c], send_idcol.at[j], recv_idcol.at[me_c], me_r, col_peer(j))

    def id_col_from(j):
        return remote(id_sum, id_col.at[col_peer(j)], send_idcol.at[j], recv_idcol.at[col_peer(j)], me_r, col_peer(j))

    def row_copy(ch, j):
        block = income.at[ch, me_r]
        return remote(block, block, send_row.at[ch, j], recv_row.at[ch, me_r], row_peer(j), me_c)

    def row_from(ch, j):
        block = income.at[ch, row_peer(j)]
        return remote(block, block, send_row.at[ch, j], recv_row.at[ch, row_peer(j)], row_peer(j), me_c)

    half = n_outer // 2
    side = outer // half
    is_gate = outer == half - 1 + side
    far_gate = (half - side) * INNER + inner

    def near(j, i):
        return (side * half + (outer % half + j) % half) * INNER + i

    def far(k, i):
        return ((1 - side) * half + k) * INNER + i

    other = INNER - 1 - inner

    def block_copy(s, source, send, peer):
        block = hidden.at[s, source]
        return remote(block, block, send, recv_hidden.at[s, source], me_r, peer)

    def await_block(s, source):
        block_copy(s, source, send_relay.at[0, source], partner).wait_recv()

    def own_copies(s):
        peers = [near(j, inner) for j in range(1, half)] + [far_gate, partner]
        return [block_copy(s, me_c, send_own.at[s % chunks, peer], peer) for peer in peers]

    def send_all(s):
        for copy in own_copies(s):
            copy.start()

    def drain_own(s):
        for copy in own_copies(s):
            copy.wait_send()

    def over(s, source):
        return block_copy(s, source, send_relay.at[s % chunks, source], partner)

    def along(s, source, j):
        return block_copy(s, source, send_along.at[s % chunks, source // INNER, j], near(j, inner))

    def pass_on(s, go, source, copies):
        if go:
            await_block(s, source)
        for copy in copies:
            if go:
                copy.start()
            else:
                copy.wait_send()

    def first_relay(s, go):
        @pl.when(is_gate)
        def _():
            for k in range(half):
                source = far(k, inner)
                pass_on(s, go, source, [along(s, source, j) for j in range(1, half)] + [over(s, source)])

        @pl.when(s % 2 == 0)
        def _():
            for j in range(1, half):
                pass_on(s, go, near(j, inner), [over(s, near(j, inner))])

        @pl.when(s % 2 == 1)
        def _():
            pass_on(s, go, partner, [along(s, partner, j) for j in range(1, half)])

    def second_relay(s, go):
        @pl.when(jnp.logical_not(is_gate))
        def _():
            for k in range(half):
                pass_on(s, go, far(k, inner), [over(s, far(k, inner))])

    def await_rest(s):
        @pl.when(s % 2 == 0)
        def _():
            await_block(s, partner)

        @pl.when(s % 2 == 1)
        def _():
            for j in range(1, half):
                await_block(s, near(j, inner))

        for j in range(1, half):
            await_block(s, near(j, other))
        for k in range(half):
            await_block(s, far(k, other))

    def relay(s, relay_of):
        @pl.when(s < steps)
        def _():
            @pl.when(s >= chunks)
            def _():
                relay_of(s - chunks, False)

            relay_of(s, True)

    for j in range(1, n_row):
        id_row_copy(j).start()
    for ch in range(chunks):
        send_all(ch)

    for l in range(layers):
        gain[l] = gain_ref[l : l + 1, :]
    out_ref[...] = jnp.zeros(out_ref.shape, BF16)
    ids_here = id_own[...]
    for j in range(1, n_row):
        id_row_from(j).wait_recv()
        ids_here = ids_here + id_row[row_peer(j)]
    id_sum[...] = ids_here
    id_col[me_c] = ids_here
    for j in range(1, n_col):
        id_col_copy(j).start()

    for s in range(LEAD1):
        first_relay(jnp.int32(s), True)
    for s in range(LEAD2):
        second_relay(jnp.int32(s), True)

    for j in range(1, n_col):
        id_col_from(j).wait_recv()
    tiles = []
    for tile in range(n_col // per_tile):
        joined = id_col[tile * per_tile]
        for c in range(tile * per_tile + 1, (tile + 1) * per_tile):
            joined = joined + id_col[c]
        tiles.append(joined)
    ids = jnp.concatenate(tiles, 1)

    bits = SUB.bit_length() - 1
    wide = (n_col * SUB).bit_length() - 1

    def origin(lane):
        group = lane >> wide
        source = (lane >> bits) & (n_col - 1)
        return source * rows_dev + group * SUB + (lane & (SUB - 1))

    low = lax.broadcasted_iota(jnp.int32, (slots, slots), 0)
    high = lax.broadcasted_iota(jnp.int32, (slots, slots), 1)
    shuffle = jnp.where(low == origin(high), 1.0, 0.0).astype(BF16)
    earlier = jnp.where(origin(low) < origin(high), 1.0, 0.0).astype(BF16)
    ids = jnp.dot(ids.astype(F32).astype(BF16), shuffle, preferred_element_type=F32).astype(jnp.int32)
    line = lax.broadcasted_iota(jnp.int32, (lead_dim, slots), 0)
    line_col = lax.broadcasted_iota(jnp.int32, (lead_dim, 1), 0)
    ids = jnp.where(line < n_row, ids, tasks)
    live = ids < tasks
    member = [jnp.where(ids == t, 1.0, 0.0) for t in range(tasks)]
    ranks = jnp.dot(jnp.concatenate(member, 0).astype(BF16), earlier, preferred_element_type=F32)
    base = jnp.zeros((1, 1), F32)
    position = jnp.zeros((lead_dim, slots), F32)
    for t in range(tasks):
        count = jnp.sum(member[t], axis=1, keepdims=True)
        offset = jnp.zeros((lead_dim, 1), F32) + base
        for r in range(n_row):
            here = count[r : r + 1, :]
            offset = offset + jnp.where(line_col > r, here, 0.0)
            base = base + here
        rank = ranks[t * lead_dim : (t + 1) * lead_dim, :]
        position = position + member[t] * (offset + rank)
    slot = jnp.floor((position + 0.5) * (1.0 / n_row))
    target = jnp.where(live, position - slot * n_row, -1.0).astype(jnp.int32)
    slot = jnp.where(target == me_r, slot.astype(jnp.int32), -1)
    slot_range = lax.broadcasted_iota(jnp.int32, (slots, n_row * m), 0)
    for ch in range(chunks):
        aimed = jnp.concatenate([slot[r : r + 1, ch * m : (ch + 1) * m] for r in range(n_row)], 1)
        put[ch] = jnp.where(slot_range == aimed, 1.0, 0.0).astype(BF16)

    def silu(values):
        half = 0.5 * values
        return (half + half * jnp.tanh(half)).astype(BF16)

    def opening(g, carry):
        for h in range(halves):
            s = g * halves + h
            relay(s + LEAD2, second_relay)
            relay(s + LEAD1, first_relay)

            @pl.when(s == 0)
            def _():
                weight_copy(0).wait()

            await_rest(s)
        for c in range(n_col):
            lines = slice(c * SUB, (c + 1) * SUB)

            def piece(p):
                return hidden[g * halves + p // span, c, (p % span) * SUB : (p % span + 1) * SUB, :].astype(F32)

            total = jnp.zeros((SUB, part), F32)
            for p in range(n_col):
                values = piece(p)
                total = total + values * values
            inverse = lax.rsqrt(jnp.sum(total, axis=1, keepdims=True) * (1.0 / width) + epsilon)
            for p in range(n_col):
                cols = slice(p * part, (p + 1) * part)
                active[lines, cols] = silu(piece(p) * inverse * gain[0, :, cols])
        update = jnp.dot(active[...], weight[0], preferred_element_type=F32)
        own_lines = pl.ds(pl.multiple_of((me_c % span) * SUB, SUB), SUB)
        for h in range(halves):
            drain_own(g * halves + h)
        for c in range(n_col):
            own = hidden[g * halves + me_c // span, c, own_lines, :].astype(F32)
            result = (own + update[c * SUB : (c + 1) * SUB, :]).astype(BF16)
            hidden[chunks + g * halves + c // span, me_c, (c % span) * SUB : (c % span + 1) * SUB, :] = result
        for h in range(halves):
            send_all(chunks + g * halves + h)
        return carry

    lax.fori_loop(0, groups, opening, 0)

    def place(ch):
        for j in range(1, n_row):
            row_from(ch, j).wait_recv()
        arrived = income[ch].reshape(n_row * m, part)
        placed = jnp.dot(put[ch], arrived, preferred_element_type=F32)
        out_ref[...] = (out_ref[...].astype(F32) + placed).astype(BF16)

    def step(s, carry):
        l = s // chunks
        ch = s % chunks
        relay(s + LEAD2, second_relay)
        relay(s + LEAD1, first_relay)

        @pl.when(ch == 0)
        def _():
            weight_copy(l).wait()

        await_rest(s)
        total = jnp.zeros((m, part), F32)
        for c in range(n_col):
            values = hidden[s, c].astype(F32)
            total = total + values * values
        mean = jnp.sum(total, axis=1, keepdims=True) * (1.0 / width)
        inverse = lax.rsqrt(mean + epsilon)
        for c in range(n_col):
            cols = slice(c * part, (c + 1) * part)
            active[:m, cols] = silu(hidden[s, c].astype(F32) * inverse * gain[l, :, cols])
        update = jnp.dot(active[:m, :], weight[l], preferred_element_type=F32)
        result = (hidden[s, me_c].astype(F32) + update).astype(BF16)

        drain_own(s)

        @pl.when(l < layers - 1)
        def _():
            hidden[s + chunks, me_c] = result
            send_all(s + chunks)

        @pl.when(l == layers - 1)
        def _():
            income[ch, me_r] = result
            for j in range(1, n_row):
                row_copy(ch, j).start()

            @pl.when(ch >= 1)
            def _():
                place(ch - 1)

        return carry

    lax.fori_loop(chunks, steps, step, 0)
    place(chunks - 1)

    for ch in range(chunks):
        first_relay(jnp.int32(steps - chunks + ch), False)
        second_relay(jnp.int32(steps - chunks + ch), False)
        for j in range(1, n_row):
            row_copy(ch, j).wait_send()
    for j in range(1, n_row):
        id_row_copy(j).wait_send()
    for j in range(1, n_col):
        id_col_copy(j).wait_send()


def shards(rows, task_ids, task_embed, norm_gain, layer_weight):
    rows_dev, width = rows.shape
    tasks = task_embed.shape[0]
    layers = layer_weight.shape[0]
    part = layer_weight.shape[2]
    n_row = lax.axis_size("row")
    n_col = lax.axis_size("col")
    slots = rows_dev * n_col
    chunks = CHUNKS
    m = slots // chunks
    lead_dim = -(-n_row // 8) * 8
    lanes = 128
    sizes = (n_row, n_col, layers, chunks, tasks)
    dma = pltpu.SemaphoreType.DMA
    vmem = pl.BlockSpec(memory_space=pltpu.VMEM)
    return pl.pallas_call(
        functools.partial(kernel, sizes),
        out_shape=jax.ShapeDtypeStruct((slots, part), BF16),
        in_specs=[vmem, vmem, vmem, vmem, pl.BlockSpec(memory_space=pl.ANY)],
        out_specs=vmem,
        scratch_shapes=[
            pltpu.VMEM((layers, width, part), BF16),
            pltpu.VMEM((layers * chunks, n_col, m, part), BF16),
            pltpu.VMEM((n_col * SUB, width), BF16),
            pltpu.VMEM((layers, 1, width), F32),
            pltpu.VMEM((chunks, n_row, m, part), BF16),
            pltpu.VMEM((chunks, slots, n_row * m), BF16),
            pltpu.VMEM((lead_dim, lanes), jnp.int32),
            pltpu.VMEM((n_row, lead_dim, lanes), jnp.int32),
            pltpu.VMEM((lead_dim, lanes), jnp.int32),
            pltpu.VMEM((n_col, lead_dim, lanes), jnp.int32),
            dma((layers,)),
            dma((n_row,)),
            dma((n_row,)),
            dma((n_col,)),
            dma((n_col,)),
            dma((chunks, n_row)),
            dma((chunks, n_row)),
            dma((chunks, n_col)),
            dma((chunks, n_col)),
            dma((chunks, n_col // INNER, max(1, n_col // INNER // 2))),
            dma((layers * chunks, n_col)),
        ],
        compiler_params=pltpu.CompilerParams(
            collective_id=0, has_side_effects=True, vmem_limit_bytes=60 * 1024 * 1024
        ),
    )(rows, task_ids.reshape(1, rows_dev), task_embed, norm_gain, layer_weight)


def solution(mesh):
    return jax.shard_map(
        shards,
        mesh=mesh,
        in_specs=(P(("row", "col"), None), P(("row", "col")), P(), P(), P(None, None, "col")),
        out_specs=P("row", "col"),
        check_vma=False,
    )
```

time: 110 us -> 103 us (0.936); the launches traced: 109 us -> 103 us
  Pallas kernels: 107 us -> 101 us
    pallas_call x1, Pallas kernels: 107 us -> 101 us  [shards(): pl.pallas_call(functools.partial(kernel, sizes), out_shape=jax.ShapeDtype...]
where the time goes in v1:
time: 103 us
  Pallas kernels  101 us (98%)
  local copies, waits for them, and re-layouts  1.67 us (2%)
    pallas_call x1, Pallas kernels, shards(): pl.pallas_call(functools.partial(kernel, sizes), out_shape=jax.ShapeDtype...  101 us

profile of v1, /device:TPU:1, one launch (start us, length us, event | category | flops | bytes accessed | tf_op | source)
XLA Modules:
  0.0 103.0 jit_solution(2854593243622576262)
XLA Ops:
  0.0 101.4 %shard_map.55 = bf16[256,512]{1,0:T(8,128)(2,1)} custom-call(bf16[32,4096]{1,0:T(8,128)(2,1)} %rows_ref.1, s32[1,32]{1,0:T(1,128)} %bitcast.1, bf16[8,4096]{1,0:T(8,128)(2,1)} %embed_ref.1, f32[4,4096]{1,0:T(4,128)} %gain_ref.1, bf16[4,4096,512]{2,1,0:T(8,128)(2,1)} %weight_ref.1), custom_call_target="tpu_custom_call" | custom-call | tf_op jit(solution)/shard_map/pallas_call | solution.py:428
  101.4 1.7 %copy.7 = bf16[256,512]{1,0:T(8,128)(2,1)} copy(bf16[256,512]{1,0:T(8,128)(2,1)} %shard_map.55) | data formatting | bytes 524288

commit v2 on v1

--- a/solution.py
+++ b/solution.py
@@ -1,4 +1,5 @@
 import functools
+import math
 
 import jax
 import jax.numpy as jnp
@@ -12,6 +13,7 @@
 INNER = 2
 CHUNKS = 4
 SUB = 16
+SPARE = 10 * 2**20
 LEAD1 = 2
 LEAD2 = 1
 F32 = jnp.float32
@@ -20,22 +22,27 @@
 
 def kernel(
     sizes,
+    rows_hbm,
+    ids_hbm,
+    embed_hbm,
+    gain_hbm,
+    weight_ref,
+    out_ref,
     rows_ref,
     ids_ref,
     embed_ref,
-    gain_ref,
-    weight_ref,
-    out_ref,
+    gain,
     weight,
     hidden,
     active,
-    gain,
     income,
     put,
     id_own,
     id_row,
     id_sum,
     id_col,
+    sem_input,
+    sem_gain,
     sem_weight,
     send_idrow,
     recv_idrow,
@@ -85,7 +92,21 @@
     for j in range(1, n_col):
         pl.semaphore_signal(barrier, inc=1, device_id=(me_r, col_peer(j)), device_id_type=MESH)
 
+    inputs = [
+        pltpu.make_async_copy(source, dest, sem_input.at[i])
+        for i, (source, dest) in enumerate(((rows_hbm, rows_ref), (embed_hbm, embed_ref), (ids_hbm, ids_ref)))
+    ]
+    for copy in inputs:
+        copy.start()
+
+    def gain_copy(l):
+        return pltpu.make_async_copy(gain_hbm.at[pl.ds(l, 1)], gain.at[l], sem_gain.at[l])
+
+    out_ref[...] = jnp.zeros(out_ref.shape, BF16)
+    for copy in inputs:
+        copy.wait()
     for l in range(layers):
+        gain_copy(l).start()
         weight_copy(l).start()
 
     lead_dim = id_own.shape[0]
@@ -239,70 +260,69 @@
     for ch in range(chunks):
         send_all(ch)
 
-    for l in range(layers):
-        gain[l] = gain_ref[l : l + 1, :]
-    out_ref[...] = jnp.zeros(out_ref.shape, BF16)
-    ids_here = id_own[...]
-    for j in range(1, n_row):
-        id_row_from(j).wait_recv()
-        ids_here = ids_here + id_row[row_peer(j)]
-    id_sum[...] = ids_here
-    id_col[me_c] = ids_here
-    for j in range(1, n_col):
-        id_col_copy(j).start()
-
     for s in range(LEAD1):
         first_relay(jnp.int32(s), True)
     for s in range(LEAD2):
         second_relay(jnp.int32(s), True)
 
-    for j in range(1, n_col):
-        id_col_from(j).wait_recv()
-    tiles = []
-    for tile in range(n_col // per_tile):
-        joined = id_col[tile * per_tile]
-        for c in range(tile * per_tile + 1, (tile + 1) * per_tile):
-            joined = joined + id_col[c]
-        tiles.append(joined)
-    ids = jnp.concatenate(tiles, 1)
-
-    bits = SUB.bit_length() - 1
-    wide = (n_col * SUB).bit_length() - 1
-
-    def origin(lane):
-        group = lane >> wide
-        source = (lane >> bits) & (n_col - 1)
-        return source * rows_dev + group * SUB + (lane & (SUB - 1))
-
-    low = lax.broadcasted_iota(jnp.int32, (slots, slots), 0)
-    high = lax.broadcasted_iota(jnp.int32, (slots, slots), 1)
-    shuffle = jnp.where(low == origin(high), 1.0, 0.0).astype(BF16)
-    earlier = jnp.where(origin(low) < origin(high), 1.0, 0.0).astype(BF16)
-    ids = jnp.dot(ids.astype(F32).astype(BF16), shuffle, preferred_element_type=F32).astype(jnp.int32)
-    line = lax.broadcasted_iota(jnp.int32, (lead_dim, slots), 0)
-    line_col = lax.broadcasted_iota(jnp.int32, (lead_dim, 1), 0)
-    ids = jnp.where(line < n_row, ids, tasks)
-    live = ids < tasks
-    member = [jnp.where(ids == t, 1.0, 0.0) for t in range(tasks)]
-    ranks = jnp.dot(jnp.concatenate(member, 0).astype(BF16), earlier, preferred_element_type=F32)
-    base = jnp.zeros((1, 1), F32)
-    position = jnp.zeros((lead_dim, slots), F32)
-    for t in range(tasks):
-        count = jnp.sum(member[t], axis=1, keepdims=True)
-        offset = jnp.zeros((lead_dim, 1), F32) + base
-        for r in range(n_row):
-            here = count[r : r + 1, :]
-            offset = offset + jnp.where(line_col > r, here, 0.0)
-            base = base + here
-        rank = ranks[t * lead_dim : (t + 1) * lead_dim, :]
-        position = position + member[t] * (offset + rank)
-    slot = jnp.floor((position + 0.5) * (1.0 / n_row))
-    target = jnp.where(live, position - slot * n_row, -1.0).astype(jnp.int32)
-    slot = jnp.where(target == me_r, slot.astype(jnp.int32), -1)
-    slot_range = lax.broadcasted_iota(jnp.int32, (slots, n_row * m), 0)
-    for ch in range(chunks):
-        aimed = jnp.concatenate([slot[r : r + 1, ch * m : (ch + 1) * m] for r in range(n_row)], 1)
-        put[ch] = jnp.where(slot_range == aimed, 1.0, 0.0).astype(BF16)
+    def pass_ids():
+        ids_here = id_own[...]
+        for j in range(1, n_row):
+            id_row_from(j).wait_recv()
+            ids_here = ids_here + id_row[row_peer(j)]
+        id_sum[...] = ids_here
+        id_col[me_c] = ids_here
+        for j in range(1, n_col):
+            id_col_copy(j).start()
+
+    def find_places():
+        for j in range(1, n_col):
+            id_col_from(j).wait_recv()
+        tiles = []
+        for tile in range(n_col // per_tile):
+            joined = id_col[tile * per_tile]
+            for c in range(tile * per_tile + 1, (tile + 1) * per_tile):
+                joined = joined + id_col[c]
+            tiles.append(joined)
+        ids = jnp.concatenate(tiles, 1)
+
+        bits = SUB.bit_length() - 1
+        wide = (n_col * SUB).bit_length() - 1
+
+        def origin(lane):
+            group = lane >> wide
+            source = (lane >> bits) & (n_col - 1)
+            return source * rows_dev + group * SUB + (lane & (SUB - 1))
+
+        low = lax.broadcasted_iota(jnp.int32, (slots, slots), 0)
+        high = lax.broadcasted_iota(jnp.int32, (slots, slots), 1)
+        shuffle = jnp.where(low == origin(high), 1.0, 0.0).astype(BF16)
+        earlier = jnp.where(origin(low) < origin(high), 1.0, 0.0).astype(BF16)
+        ids = jnp.dot(ids.astype(F32).astype(BF16), shuffle, preferred_element_type=F32).astype(jnp.int32)
+        line = lax.broadcasted_iota(jnp.int32, (lead_dim, slots), 0)
+        line_col = lax.broadcasted_iota(jnp.int32, (lead_dim, 1), 0)
+        ids = jnp.where(line < n_row, ids, tasks)
+        live = ids < tasks
+        member = [jnp.where(ids == t, 1.0, 0.0) for t in range(tasks)]
+        ranks = jnp.dot(jnp.concatenate(member, 0).astype(BF16), earlier, preferred_element_type=F32)
+        base = jnp.zeros((1, 1), F32)
+        position = jnp.zeros((lead_dim, slots), F32)
+        for t in range(tasks):
+            count = jnp.sum(member[t], axis=1, keepdims=True)
+            offset = jnp.zeros((lead_dim, 1), F32) + base
+            for r in range(n_row):
+                here = count[r : r + 1, :]
+                offset = offset + jnp.where(line_col > r, here, 0.0)
+                base = base + here
+            rank = ranks[t * lead_dim : (t + 1) * lead_dim, :]
+            position = position + member[t] * (offset + rank)
+        slot = jnp.floor((position + 0.5) * (1.0 / n_row))
+        target = jnp.where(live, position - slot * n_row, -1.0).astype(jnp.int32)
+        slot = jnp.where(target == me_r, slot.astype(jnp.int32), -1)
+        slot_range = lax.broadcasted_iota(jnp.int32, (slots, n_row * m), 0)
+        for ch in range(chunks):
+            aimed = jnp.concatenate([slot[r : r + 1, ch * m : (ch + 1) * m] for r in range(n_row)], 1)
+            put[ch] = jnp.where(slot_range == aimed, 1.0, 0.0).astype(BF16)
 
     def silu(values):
         half = 0.5 * values
@@ -317,6 +337,8 @@
             @pl.when(s == 0)
             def _():
                 weight_copy(0).wait()
+                for l in range(layers):
+                    gain_copy(l).wait()
 
             await_rest(s)
         for c in range(n_col):
@@ -394,20 +416,30 @@
             def _():
                 place(ch - 1)
 
+        @pl.when(s == chunks)
+        def _():
+            pass_ids()
+
+        @pl.when(s == 2 * chunks)
+        def _():
+            find_places()
+
         return carry
 
     lax.fori_loop(chunks, steps, step, 0)
-    place(chunks - 1)
-
     for ch in range(chunks):
         first_relay(jnp.int32(steps - chunks + ch), False)
         second_relay(jnp.int32(steps - chunks + ch), False)
-        for j in range(1, n_row):
-            row_copy(ch, j).wait_send()
     for j in range(1, n_row):
         id_row_copy(j).wait_send()
     for j in range(1, n_col):
         id_col_copy(j).wait_send()
+    for ch in range(chunks - 1):
+        for j in range(1, n_row):
+            row_copy(ch, j).wait_send()
+    place(chunks - 1)
+    for j in range(1, n_row):
+        row_copy(chunks - 1, j).wait_send()
 
 
 def shards(rows, task_ids, task_embed, norm_gain, layer_weight):
@@ -423,24 +455,35 @@
     lead_dim = -(-n_row // 8) * 8
     lanes = 128
     sizes = (n_row, n_col, layers, chunks, tasks)
+    buffers = [
+        pltpu.VMEM((rows_dev, width), BF16),
+        pltpu.VMEM((1, rows_dev), jnp.int32),
+        pltpu.VMEM((tasks, width), BF16),
+        pltpu.VMEM((layers, 1, width), F32),
+        pltpu.VMEM((layers, width, part), BF16),
+        pltpu.VMEM((layers * chunks, n_col, m, part), BF16),
+        pltpu.VMEM((n_col * SUB, width), BF16),
+        pltpu.VMEM((chunks, n_row, m, part), BF16),
+        pltpu.VMEM((chunks, slots, n_row * m), BF16),
+        pltpu.VMEM((lead_dim, lanes), jnp.int32),
+        pltpu.VMEM((n_row, lead_dim, lanes), jnp.int32),
+        pltpu.VMEM((lead_dim, lanes), jnp.int32),
+        pltpu.VMEM((n_col, lead_dim, lanes), jnp.int32),
+    ]
+    held = sum(math.prod(b.shape) * jnp.dtype(b.dtype).itemsize for b in buffers)
     dma = pltpu.SemaphoreType.DMA
     vmem = pl.BlockSpec(memory_space=pltpu.VMEM)
+    hbm = pl.BlockSpec(memory_space=pltpu.HBM)
+    operands = [rows, task_ids.reshape(1, rows_dev), task_embed, norm_gain, layer_weight]
     return pl.pallas_call(
         functools.partial(kernel, sizes),
         out_shape=jax.ShapeDtypeStruct((slots, part), BF16),
-        in_specs=[vmem, vmem, vmem, vmem, pl.BlockSpec(memory_space=pl.ANY)],
+        in_specs=[hbm] * 5,
         out_specs=vmem,
-        scratch_shapes=[
-            pltpu.VMEM((layers, width, part), BF16),
-            pltpu.VMEM((layers * chunks, n_col, m, part), BF16),
-            pltpu.VMEM((n_col * SUB, width), BF16),
-            pltpu.VMEM((layers, 1, width), F32),
-            pltpu.VMEM((chunks, n_row, m, part), BF16),
-            pltpu.VMEM((chunks, slots, n_row * m), BF16),
-            pltpu.VMEM((lead_dim, lanes), jnp.int32),
-            pltpu.VMEM((n_row, lead_dim, lanes), jnp.int32),
-            pltpu.VMEM((lead_dim, lanes), jnp.int32),
-            pltpu.VMEM((n_col, lead_dim, lanes), jnp.int32),
+        scratch_shapes=buffers
+        + [
+            dma((3,)),
+            dma((layers,)),
             dma((layers,)),
             dma((n_row,)),
             dma((n_row,)),
@@ -454,9 +497,9 @@
             dma((layers * chunks, n_col)),
         ],
         compiler_params=pltpu.CompilerParams(
-            collective_id=0, has_side_effects=True, vmem_limit_bytes=60 * 1024 * 1024
+            collective_id=0, has_side_effects=True, vmem_limit_bytes=min(held + SPARE, 60 * 2**20)
         ),
-    )(rows, task_ids.reshape(1, rows_dev), task_embed, norm_gain, layer_weight)
+    )(*[pltpu.with_memory_space_constraint(operand, pltpu.HBM) for operand in operands])
 
 
 def solution(mesh):

time: 103 us -> 98.7 us (0.958)
  Pallas kernels: 101 us -> 97.9 us
    pallas_call x1, Pallas kernels: 101 us -> 97.9 us  [shards(): pl.pallas_call(functools.partial(kernel, sizes), out_shape=jax.ShapeDtype...]
where the time goes in v2:
time: 98.7 us; the launch traced here: 98.6 us
  Pallas kernels  97.9 us (99%)
    pallas_call x1, Pallas kernels, shards(): pl.pallas_call(functools.partial(kernel, sizes), out_shape=jax.ShapeDtype...  97.9 us

profile of v2, /device:TPU:1, one launch (start us, length us, event | category | flops | bytes accessed | tf_op | source)
XLA Modules:
  0.0 98.6 jit_solution(2297283262568868591)
XLA Ops:
  0.0 97.9 %shard_map.55 = bf16[256,512]{1,0:T(8,128)(2,1)S(1)} custom-call(bf16[32,4096]{1,0:T(8,128)(2,1)} %rows_hbm.1, s32[1,32]{1,0:T(1,128)} %bitcast.1, bf16[8,4096]{1,0:T(8,128)(2,1)} %embed_hbm.1, f32[4,4096]{1,0:T(4,128)} %gain_hbm.1, bf16[4,4096,512]{2,1,0:T(8,128)(2,1)} %weight_ref.1), custom_call_target="tpu_custom_call" | custom-call | tf_op jit(solution)/shard_map/pallas_call | solution.py:478
  97.9 0.7 copy.7

commit v3 on v2

--- a/solution.py
+++ b/solution.py
@@ -16,6 +16,9 @@
 SPARE = 10 * 2**20
 LEAD1 = 2
 LEAD2 = 1
+SHIP = {1: (0,), 4: (1,), 6: (2,), 8: (3,)}
+SPREAD = {4: (0,), 6: (1,), 8: (2,), 10: (3,)}
+RELAY = {5: (0,), 7: (1,), 9: (2,), 11: (3,)}
 F32 = jnp.float32
 BF16 = jnp.bfloat16
 
@@ -37,6 +40,11 @@
     active,
     income,
     put,
+    helped,
+    part_out,
+    part_in,
+    scale_out,
+    scale_in,
     id_own,
     id_row,
     id_sum,
@@ -54,8 +62,14 @@
     send_relay,
     send_along,
     recv_hidden,
+    send_help,
+    recv_help,
+    send_part,
+    recv_part,
+    send_scale,
+    recv_scale,
 ):
-    n_row, n_col, layers, chunks, tasks = sizes
+    n_row, n_col, layers, chunks, tasks, assisted = sizes
     n_outer = n_col // INNER
     rows_dev = rows_ref.shape[0]
     width = rows_ref.shape[1]
@@ -63,6 +77,8 @@
     slots = rows_dev * n_col
     m = slots // chunks
     steps = layers * chunks
+    first_helped = layers - assisted
+    bound = first_helped * chunks
     groups = rows_dev // SUB
     halves = chunks // groups
     span = n_col // halves
@@ -71,6 +87,9 @@
     outer = me_c // INNER
     inner = me_c % INNER
     partner = outer * INNER + (INNER - 1 - inner)
+
+    def columns(c):
+        return pl.ds(pl.multiple_of(c * part, part), part)
 
     def col_peer(j):
         return (me_c + j) % n_col
@@ -183,22 +202,30 @@
         block_copy(s, source, send_relay.at[0, source], partner).wait_recv()
 
     def own_copies(s):
-        peers = [near(j, inner) for j in range(1, half)] + [far_gate, partner]
+        peers = [near(j, inner) for j in range(1, half)] + [partner]
         return [block_copy(s, me_c, send_own.at[s % chunks, peer], peer) for peer in peers]
+
+    def far_copy(s):
+        return block_copy(s, me_c, send_own.at[s % chunks, far_gate], far_gate)
 
     def send_all(s):
         for copy in own_copies(s):
             copy.start()
+        far_copy(s).start()
 
     def drain_own(s):
         for copy in own_copies(s):
             copy.wait_send()
+        far_copy(s).wait_send()
 
     def over(s, source):
         return block_copy(s, source, send_relay.at[s % chunks, source], partner)
 
     def along(s, source, j):
         return block_copy(s, source, send_along.at[s % chunks, source // INNER, j], near(j, inner))
+
+    def across(s, source):
+        return block_copy(s, source, send_along.at[s % chunks, source // INNER, 0], far_gate)
 
     def pass_on(s, go, source, copies):
         if go:
@@ -209,34 +236,77 @@
             else:
                 copy.wait_send()
 
-    def first_relay(s, go):
+    mate = near(1, inner)
+    far_corner = far(1 - side, inner) if half == 2 else far_gate
+    even_of = lambda s: s % 2 == 0
+    odd_of = lambda s: s % 2 == 1
+
+    def full_first(s, go):
         @pl.when(is_gate)
         def _():
             for k in range(half):
                 source = far(k, inner)
                 pass_on(s, go, source, [along(s, source, j) for j in range(1, half)] + [over(s, source)])
 
-        @pl.when(s % 2 == 0)
+        @pl.when(even_of(s))
         def _():
             for j in range(1, half):
                 pass_on(s, go, near(j, inner), [over(s, near(j, inner))])
 
-        @pl.when(s % 2 == 1)
+        @pl.when(odd_of(s))
         def _():
             pass_on(s, go, partner, [along(s, partner, j) for j in range(1, half)])
 
-    def second_relay(s, go):
+    def full_second(s, go):
         @pl.when(jnp.logical_not(is_gate))
         def _():
             for k in range(half):
                 pass_on(s, go, far(k, inner), [over(s, far(k, inner))])
 
+    def helped_first(s, go):
+        @pl.when(jnp.logical_not(is_gate))
+        def _():
+            pass_on(s, go, partner, [along(s, partner, 1)])
+            pass_on(s, go, mate, [over(s, mate)])
+
+        @pl.when(is_gate & odd_of(s))
+        def _():
+            pass_on(s, go, partner, [across(s, partner)])
+
+    def helped_second(s, go):
+        @pl.when(is_gate & even_of(s))
+        def _():
+            pass_on(s, go, far_gate, [over(s, far_gate)])
+
+        @pl.when(is_gate)
+        def _():
+            pass_on(s, go, far_corner, [over(s, far_corner)])
+
+    def either(s, full, helped_one, go):
+        if not assisted:
+            full(s, go)
+            return
+
+        @pl.when(s < bound)
+        def _():
+            full(s, go)
+
+        @pl.when(s >= bound)
+        def _():
+            helped_one(s, go)
+
+    def first_relay(s, go):
+        either(s, full_first, helped_first, go)
+
+    def second_relay(s, go):
+        either(s, full_second, helped_second, go)
+
     def await_rest(s):
-        @pl.when(s % 2 == 0)
+        @pl.when(even_of(s))
         def _():
             await_block(s, partner)
 
-        @pl.when(s % 2 == 1)
+        @pl.when(odd_of(s))
         def _():
             for j in range(1, half):
                 await_block(s, near(j, inner))
@@ -245,6 +315,101 @@
             await_block(s, near(j, other))
         for k in range(half):
             await_block(s, far(k, other))
+
+    def await_helped(s):
+        @pl.when(is_gate & even_of(s))
+        def _():
+            await_block(s, partner)
+
+        @pl.when(is_gate & odd_of(s))
+        def _():
+            await_block(s, far_gate)
+
+        await_block(s, near(1, other))
+
+        @pl.when(is_gate)
+        def _():
+            await_block(s, mate)
+            for k in range(half):
+                await_block(s, far(k, other))
+
+    far_base = (1 - side) * (width // 2)
+    near_base = side * (width // 2)
+    share = width // 2 // n_row
+    bite = share // chunks
+    sibling = me_r + 1 - 2 * (me_r % 2)
+    cross = (me_r + 2) % n_row
+
+    def helped_part(i, q):
+        return helped.at[i // chunks, q, pl.ds((i % chunks) * bite, bite), :]
+
+    def ship_copy(i):
+        lines = pl.ds(pl.multiple_of(far_base + me_r * share + (i % chunks) * bite, bite), bite)
+        source = weight.at[first_helped + i // chunks, lines, :]
+        return remote(source, helped_part(i, me_r), send_help.at[i, 0], recv_help.at[i, me_r], me_r, mate)
+
+    def help_copy(i, q, way, peer):
+        block = helped_part(i, q)
+        return remote(block, block, send_help.at[i, way], recv_help.at[i, q], peer, me_c)
+
+    def spread_copies(i):
+        return [help_copy(i, me_r, 1, sibling), help_copy(i, me_r, 2, cross)]
+
+    def part_copy(s):
+        slot = s - bound
+        return remote(
+            part_out.at[s % chunks], part_in.at[slot], send_part.at[s % chunks], recv_part.at[slot], me_r, mate
+        )
+
+    def scale_copy(s):
+        slot = s - bound
+        return remote(
+            scale_out.at[s % chunks], scale_in.at[slot], send_scale.at[s % chunks], recv_scale.at[slot], me_r, mate
+        )
+
+    def at_steps(s, table, action):
+        for when, items in table.items():
+            @pl.when(s == when)
+            def _():
+                for i in items:
+                    action(i)
+
+    def spread(i):
+        help_copy(i, me_r, 1, sibling).wait_recv()
+        for copy in spread_copies(i):
+            copy.start()
+
+    def pass_cross(i):
+        help_copy(i, cross, 3, sibling).wait_recv()
+        help_copy(i, cross, 3, sibling).start()
+
+    def move_weights(s):
+        @pl.when(is_gate)
+        def _():
+            at_steps(s, RELAY, pass_cross)
+            at_steps(s, SPREAD, spread)
+
+        @pl.when(jnp.logical_not(is_gate))
+        def _():
+            at_steps(s, SHIP, lambda i: ship_copy(i).start())
+
+    def await_weights(l):
+        for i in range(assisted * chunks):
+            @pl.when(is_gate & (l == first_helped + i // chunks))
+            def _():
+                for q in (sibling, (cross + 1 - 2 * (me_r % 2))):
+                    help_copy(i, q, 1, sibling).wait_recv()
+
+    def drain_weights():
+        for i in range(assisted * chunks):
+            @pl.when(is_gate)
+            def _():
+                for copy in spread_copies(i) + [help_copy(i, cross, 3, sibling)]:
+                    copy.wait_send()
+
+            @pl.when(jnp.logical_not(is_gate))
+            def _():
+                ship_copy(i).wait_send()
 
     def relay(s, relay_of):
         @pl.when(s < steps)
@@ -329,18 +494,33 @@
         return (half + half * jnp.tanh(half)).astype(BF16)
 
     def opening(g, carry):
+        if assisted:
+            @pl.when(g == 0)
+            def _():
+                for l in range(first_helped, layers):
+                    weight_copy(l).wait()
+
+            @pl.when(jnp.logical_not(is_gate))
+            def _():
+                at_steps(g, {g: SHIP[g] for g in SHIP if g < groups}, lambda i: ship_copy(i).start())
+
+        @pl.when(g == 0)
+        def _():
+            for s in range(LEAD1, chunks):
+                first_relay(jnp.int32(s), True)
+            weight_copy(0).wait()
+            for l in range(layers):
+                gain_copy(l).wait()
+
         for h in range(halves):
-            s = g * halves + h
-            relay(s + LEAD2, second_relay)
-            relay(s + LEAD1, first_relay)
-
-            @pl.when(s == 0)
-            def _():
-                weight_copy(0).wait()
-                for l in range(layers):
-                    gain_copy(l).wait()
-
-            await_rest(s)
+            if h > 0:
+                second_relay(g * halves + h, True)
+            else:
+                @pl.when(g > 0)
+                def _():
+                    second_relay(g * halves, True)
+        for h in range(halves):
+            await_rest(g * halves + h)
         for c in range(n_col):
             lines = slice(c * SUB, (c + 1) * SUB)
 
@@ -365,9 +545,18 @@
             hidden[chunks + g * halves + c // span, me_c, (c % span) * SUB : (c % span + 1) * SUB, :] = result
         for h in range(halves):
             send_all(chunks + g * halves + h)
+        if assisted:
+            @pl.when(is_gate)
+            def _():
+                at_steps(g, {g: SPREAD[g] for g in SPREAD if g < groups}, spread)
+
         return carry
 
     lax.fori_loop(0, groups, opening, 0)
+    for s in range(LEAD1):
+        relay(jnp.int32(chunks + s), first_relay)
+    for s in range(LEAD2):
+        relay(jnp.int32(chunks + s), second_relay)
 
     def place(ch):
         for j in range(1, n_row):
@@ -376,13 +565,40 @@
         placed = jnp.dot(put[ch], arrived, preferred_element_type=F32)
         out_ref[...] = (out_ref[...].astype(F32) + placed).astype(BF16)
 
+    def finish(s, l, ch, result):
+        drain_own(s)
+
+        @pl.when(l < layers - 1)
+        def _():
+            hidden[s + chunks, me_c] = result
+            send_all(s + chunks)
+
+        @pl.when(l == layers - 1)
+        def _():
+            income[ch, me_r] = result
+            for j in range(1, n_row):
+                row_copy(ch, j).start()
+
+    def after(s, l, ch):
+        @pl.when((l == layers - 1) & (ch >= 1))
+        def _():
+            place(ch - 1)
+
+        @pl.when(s == chunks)
+        def _():
+            pass_ids()
+
+        @pl.when(s == 2 * chunks)
+        def _():
+            find_places()
+
     def step(s, carry):
         l = s // chunks
         ch = s % chunks
         relay(s + LEAD2, second_relay)
         relay(s + LEAD1, first_relay)
 
-        @pl.when(ch == 0)
+        @pl.when((ch == 0) & (l < first_helped) if assisted else ch == 0)
         def _():
             weight_copy(l).wait()
 
@@ -398,35 +614,78 @@
             active[:m, cols] = silu(hidden[s, c].astype(F32) * inverse * gain[l, :, cols])
         update = jnp.dot(active[:m, :], weight[l], preferred_element_type=F32)
         result = (hidden[s, me_c].astype(F32) + update).astype(BF16)
-
-        drain_own(s)
-
-        @pl.when(l < layers - 1)
-        def _():
-            hidden[s + chunks, me_c] = result
-            send_all(s + chunks)
-
-        @pl.when(l == layers - 1)
-        def _():
-            income[ch, me_r] = result
-            for j in range(1, n_row):
-                row_copy(ch, j).start()
-
-            @pl.when(ch >= 1)
-            def _():
-                place(ch - 1)
-
-        @pl.when(s == chunks)
-        def _():
-            pass_ids()
-
-        @pl.when(s == 2 * chunks)
-        def _():
-            find_places()
-
+        finish(s, l, ch, result)
+        if assisted:
+            move_weights(s)
+        after(s, l, ch)
         return carry
 
-    lax.fori_loop(chunks, steps, step, 0)
+    near_cols = pl.ds(pl.multiple_of(near_base, width // 2), width // 2)
+    far_cols = pl.ds(pl.multiple_of(far_base, width // 2), width // 2)
+
+    def activate(s, l, begin, inverse):
+        for q in range(n_col // 2):
+            c = begin * (n_col // 2) + q
+            cols = columns(c)
+            active[:m, cols] = silu(hidden[s, c].astype(F32) * inverse * gain[l, :, cols])
+
+    def helped_step(s, carry):
+        l = s // chunks
+        ch = s % chunks
+        square = lax.broadcasted_iota(jnp.int32, (m, m), 0) == lax.broadcasted_iota(jnp.int32, (m, m), 1)
+        relay(s + LEAD2, second_relay)
+        relay(s + LEAD1, first_relay)
+
+        @pl.when(ch == 0)
+        def _():
+            await_weights(l)
+
+        await_helped(s)
+
+        @pl.when(is_gate)
+        def _():
+            total = jnp.zeros((m, part), F32)
+            for c in range(n_col):
+                values = hidden[s, c].astype(F32)
+                total = total + values * values
+            mean = jnp.sum(total, axis=1, keepdims=True) * (1.0 / width)
+            inverse = lax.rsqrt(mean + epsilon)
+
+            @pl.when(s >= bound + chunks)
+            def _():
+                scale_copy(s - chunks).wait_send()
+                part_copy(s - chunks).wait_send()
+
+            scale_out[ch, 0:1, 0:m] = jnp.sum(jnp.where(square, inverse, 0.0), axis=0, keepdims=True)
+            scale_copy(s).start()
+            activate(s, l, 1 - side, inverse)
+            theirs = helped[l - first_helped].reshape(width // 2, part)
+            part_out[ch] = jnp.dot(active[:m, far_cols], theirs, preferred_element_type=F32).astype(BF16)
+            part_copy(s).start()
+            activate(s, l, side, inverse)
+            update = jnp.dot(active[:m, :], weight[l], preferred_element_type=F32)
+            finish(s, l, ch, (hidden[s, me_c].astype(F32) + update).astype(BF16))
+
+        @pl.when(jnp.logical_not(is_gate))
+        def _():
+            scale_copy(s).wait_recv()
+            inverse = jnp.sum(jnp.where(square, scale_in[s - bound, 0:1, 0:m], 0.0), axis=1, keepdims=True)
+            activate(s, l, side, inverse)
+            update = jnp.dot(active[:m, near_cols], weight[l, near_cols, :], preferred_element_type=F32)
+            part_copy(s).wait_recv()
+            update = update + part_in[s - bound].astype(F32)
+            finish(s, l, ch, (hidden[s, me_c].astype(F32) + update).astype(BF16))
+
+        @pl.when(s == steps - 2)
+        def _():
+            drain_weights()
+
+        after(s, l, ch)
+        return carry
+
+    lax.fori_loop(chunks, bound, step, 0)
+    if assisted:
+        lax.fori_loop(bound, steps, helped_step, 0)
     for ch in range(chunks):
         first_relay(jnp.int32(steps - chunks + ch), False)
         second_relay(jnp.int32(steps - chunks + ch), False)
@@ -434,6 +693,13 @@
         id_row_copy(j).wait_send()
     for j in range(1, n_col):
         id_col_copy(j).wait_send()
+    if assisted:
+        @pl.when(is_gate)
+        def _():
+            for ch in range(chunks):
+                scale_copy(steps - chunks + ch).wait_send()
+                part_copy(steps - chunks + ch).wait_send()
+
     for ch in range(chunks - 1):
         for j in range(1, n_row):
             row_copy(ch, j).wait_send()
@@ -454,7 +720,9 @@
     m = slots // chunks
     lead_dim = -(-n_row // 8) * 8
     lanes = 128
-    sizes = (n_row, n_col, layers, chunks, tasks)
+    assisted = 1 if n_col // INNER == 4 and n_row == 4 and chunks == 4 and layers >= 4 and m <= 128 else 0
+    sizes = (n_row, n_col, layers, chunks, tasks, assisted)
+    spots = max(assisted * chunks, 1)
     buffers = [
         pltpu.VMEM((rows_dev, width), BF16),
         pltpu.VMEM((1, rows_dev), jnp.int32),
@@ -465,6 +733,11 @@
         pltpu.VMEM((n_col * SUB, width), BF16),
         pltpu.VMEM((chunks, n_row, m, part), BF16),
         pltpu.VMEM((chunks, slots, n_row * m), BF16),
+        pltpu.VMEM((max(assisted, 1), n_row, width // 2 // n_row if assisted else 16, part), BF16),
+        pltpu.VMEM((chunks, m, part), BF16),
+        pltpu.VMEM((spots, m, part), BF16),
+        pltpu.VMEM((chunks, 8, lanes), F32),
+        pltpu.VMEM((spots, 8, lanes), F32),
         pltpu.VMEM((lead_dim, lanes), jnp.int32),
         pltpu.VMEM((n_row, lead_dim, lanes), jnp.int32),
         pltpu.VMEM((lead_dim, lanes), jnp.int32),
@@ -495,6 +768,12 @@
             dma((chunks, n_col)),
             dma((chunks, n_col // INNER, max(1, n_col // INNER // 2))),
             dma((layers * chunks, n_col)),
+            dma((spots, 4)),
+            dma((spots, n_row)),
+            dma((chunks,)),
+            dma((spots,)),
+            dma((chunks,)),
+            dma((spots,)),
         ],
         compiler_params=pltpu.CompilerParams(
             collective_id=0, has_side_effects=True, vmem_limit_bytes=min(held + SPARE, 60 * 2**20)

time: 98.7 us -> 98.9 us (level)
  no operation moved by 1% of the time
where the time goes in v3:
time: 98.9 us; the launch traced here: 98.8 us
  Pallas kernels  98.1 us (99%)
    pallas_call x1, Pallas kernels, shards(): pl.pallas_call(functools.partial(kernel, sizes), out_shape=jax.ShapeDtype...  98.1 us

profile of v3, /device:TPU:1, one launch (start us, length us, event | category | flops | bytes accessed | tf_op | source)
XLA Modules:
  0.0 98.8 jit_solution(173085547669812864)
XLA Ops:
  0.0 98.1 %shard_map.55 = bf16[256,512]{1,0:T(8,128)(2,1)S(1)} custom-call(bf16[32,4096]{1,0:T(8,128)(2,1)} %rows_hbm.1, s32[1,32]{1,0:T(1,128)} %bitcast.1, bf16[8,4096]{1,0:T(8,128)(2,1)} %embed_hbm.1, f32[4,4096]{1,0:T(4,128)} %gain_hbm.1, bf16[4,4096,512]{2,1,0:T(8,128)(2,1)} %weight_ref.1), custom_call_target="tpu_custom_call" | custom-call | tf_op jit(solution)/shard_map/pallas_call | solution.py:751
  98.1 0.7 copy.7

commit v4 on v3

--- a/solution.py
+++ b/solution.py
@@ -16,9 +16,9 @@
 SPARE = 10 * 2**20
 LEAD1 = 2
 LEAD2 = 1
-SHIP = {1: (0,), 4: (1,), 6: (2,), 8: (3,)}
-SPREAD = {4: (0,), 6: (1,), 8: (2,), 10: (3,)}
-RELAY = {5: (0,), 7: (1,), 9: (2,), 11: (3,)}
+SHIP = {0: (0,), 1: (1,), 5: (2,), 8: (3,)}
+SPREAD = {1: (0,), 4: (1,), 7: (2,), 9: (3,)}
+RELAY = {5: (0,), 6: (1,), 9: (2,), 11: (3,)}
 F32 = jnp.float32
 BF16 = jnp.bfloat16
 
@@ -196,33 +196,36 @@
 
     def block_copy(s, source, send, peer):
         block = hidden.at[s, source]
-        return remote(block, block, send, recv_hidden.at[s, source], me_r, peer)
+        return remote(block, block, send, recv_hidden.at[s % (2 * chunks), source], me_r, peer)
 
     def await_block(s, source):
-        block_copy(s, source, send_relay.at[0, source], partner).wait_recv()
+        block_copy(s, source, send_relay.at[0, 0], partner).wait_recv()
+
+    def near_copies(s):
+        return [block_copy(s, me_c, send_own.at[s % chunks, j], near(j, inner)) for j in range(1, half)]
+
+    def other_copies(s):
+        return [
+            block_copy(s, me_c, send_own.at[s % chunks, 0], partner),
+            block_copy(s, me_c, send_own.at[s % chunks, half], far_gate),
+        ]
 
     def own_copies(s):
-        peers = [near(j, inner) for j in range(1, half)] + [partner]
-        return [block_copy(s, me_c, send_own.at[s % chunks, peer], peer) for peer in peers]
-
-    def far_copy(s):
-        return block_copy(s, me_c, send_own.at[s % chunks, far_gate], far_gate)
+        return near_copies(s) + other_copies(s)
 
     def send_all(s):
         for copy in own_copies(s):
             copy.start()
-        far_copy(s).start()
 
     def drain_own(s):
         for copy in own_copies(s):
             copy.wait_send()
-        far_copy(s).wait_send()
 
     def over(s, source):
-        return block_copy(s, source, send_relay.at[s % chunks, source], partner)
+        return block_copy(s, source, send_relay.at[s % chunks, source // INNER], partner)
 
     def along(s, source, j):
-        return block_copy(s, source, send_along.at[s % chunks, source // INNER, j], near(j, inner))
+        return block_copy(s, source, send_along.at[s % chunks, source // INNER, j - 1], near(j, inner))
 
     def across(s, source):
         return block_copy(s, source, send_along.at[s % chunks, source // INNER, 0], far_gate)
@@ -521,6 +524,15 @@
                     second_relay(g * halves, True)
         for h in range(halves):
             await_rest(g * halves + h)
+
+        @pl.when(g == groups - 1)
+        def _():
+            relay(jnp.int32(chunks), first_relay)
+
+            @pl.when(is_gate)
+            def _():
+                relay(jnp.int32(chunks + 1), first_relay)
+
         for c in range(n_col):
             lines = slice(c * SUB, (c + 1) * SUB)
 
@@ -553,8 +565,10 @@
         return carry
 
     lax.fori_loop(0, groups, opening, 0)
-    for s in range(LEAD1):
-        relay(jnp.int32(chunks + s), first_relay)
+    @pl.when(jnp.logical_not(is_gate))
+    def _():
+        relay(jnp.int32(chunks + 1), first_relay)
+
     for s in range(LEAD2):
         relay(jnp.int32(chunks + s), second_relay)
 
@@ -580,9 +594,9 @@
                 row_copy(ch, j).start()
 
     def after(s, l, ch):
-        @pl.when((l == layers - 1) & (ch >= 1))
-        def _():
-            place(ch - 1)
+        @pl.when((l == layers - 1) & (ch >= 2))
+        def _():
+            place(ch - 2)
 
         @pl.when(s == chunks)
         def _():
@@ -703,6 +717,7 @@
     for ch in range(chunks - 1):
         for j in range(1, n_row):
             row_copy(ch, j).wait_send()
+    place(chunks - 2)
     place(chunks - 1)
     for j in range(1, n_row):
         row_copy(chunks - 1, j).wait_send()
@@ -764,10 +779,10 @@
             dma((n_col,)),
             dma((chunks, n_row)),
             dma((chunks, n_row)),
-            dma((chunks, n_col)),
-            dma((chunks, n_col)),
-            dma((chunks, n_col // INNER, max(1, n_col // INNER // 2))),
-            dma((layers * chunks, n_col)),
+            dma((chunks, n_col // INNER // 2 + 1)),
+            dma((chunks, n_col // INNER)),
+            dma((chunks, n_col // INNER, max(1, n_col // INNER // 2 - 1))),
+            dma((2 * chunks, n_col)),
             dma((spots, 4)),
             dma((spots, n_row)),
             dma((chunks,)),

time: 98.9 us -> 95.8 us (0.969)
  Pallas kernels: 98.1 us -> 95 us
    pallas_call x1, Pallas kernels: 98.1 us -> 95 us  [shards(): pl.pallas_call(functools.partial(kernel, sizes), out_shape=jax.ShapeDtype...]
where the time goes in v4:
time: 95.8 us; the launch traced here: 95.7 us
  Pallas kernels  95 us (99%)
    pallas_call x1, Pallas kernels, shards(): pl.pallas_call(functools.partial(kernel, sizes), out_shape=jax.ShapeDtype...  95 us

profile of v4, /device:TPU:1, one launch (start us, length us, event | category | flops | bytes accessed | tf_op | source)
XLA Modules:
  0.0 95.7 jit_solution(3221256966914448443)
XLA Ops:
  0.0 95.0 %shard_map.55 = bf16[256,512]{1,0:T(8,128)(2,1)S(1)} custom-call(bf16[32,4096]{1,0:T(8,128)(2,1)} %rows_hbm.1, s32[1,32]{1,0:T(1,128)} %bitcast.1, bf16[8,4096]{1,0:T(8,128)(2,1)} %embed_hbm.1, f32[4,4096]{1,0:T(4,128)} %gain_hbm.1, bf16[4,4096,512]{2,1,0:T(8,128)(2,1)} %weight_ref.1), custom_call_target="tpu_custom_call" | custom-call | tf_op jit(solution)/shard_map/pallas_call | solution.py:766
  95.0 0.7 copy.7

commit v5 on v4

--- a/solution.py
+++ b/solution.py
@@ -16,9 +16,9 @@
 SPARE = 10 * 2**20
 LEAD1 = 2
 LEAD2 = 1
-SHIP = {0: (0,), 1: (1,), 5: (2,), 8: (3,)}
-SPREAD = {1: (0,), 4: (1,), 7: (2,), 9: (3,)}
-RELAY = {5: (0,), 6: (1,), 9: (2,), 11: (3,)}
+SHIP = {0: (0,), 1: (1, 2), 5: (3,)}
+SPREAD = {1: (0,), 4: (1,), 6: (2,), 9: (3,)}
+RELAY = {5: (0,), 6: (1,), 8: (2,), 11: (3,)}
 F32 = jnp.float32
 BF16 = jnp.bfloat16
 

time: 95.8 us -> 95 us (level)
  no operation moved by 1% of the time
where the time goes in v5:
time: 95 us; the launch traced here: 94.8 us
  Pallas kernels  94.1 us (99%)
    pallas_call x1, Pallas kernels, shards(): pl.pallas_call(functools.partial(kernel, sizes), out_shape=jax.ShapeDtype...  94.1 us

profile of v5, /device:TPU:1, one launch (start us, length us, event | category | flops | bytes accessed | tf_op | source)
XLA Modules:
  0.0 94.8 jit_solution(16588968724109905258)
XLA Ops:
  0.0 94.1 %shard_map.55 = bf16[256,512]{1,0:T(8,128)(2,1)S(1)} custom-call(bf16[32,4096]{1,0:T(8,128)(2,1)} %rows_hbm.1, s32[1,32]{1,0:T(1,128)} %bitcast.1, bf16[8,4096]{1,0:T(8,128)(2,1)} %embed_hbm.1, f32[4,4096]{1,0:T(4,128)} %gain_hbm.1, bf16[4,4096,512]{2,1,0:T(8,128)(2,1)} %weight_ref.1), custom_call_target="tpu_custom_call" | custom-call | tf_op jit(solution)/shard_map/pallas_call | solution.py:766
  94.1 0.7 copy.7

commit v6 on v5

--- a/solution.py
+++ b/solution.py
@@ -206,12 +206,12 @@
 
     def other_copies(s):
         return [
+            block_copy(s, me_c, send_own.at[s % chunks, half], far_gate),
             block_copy(s, me_c, send_own.at[s % chunks, 0], partner),
-            block_copy(s, me_c, send_own.at[s % chunks, half], far_gate),
         ]
 
     def own_copies(s):
-        return near_copies(s) + other_copies(s)
+        return other_copies(s) + near_copies(s)
 
     def send_all(s):
         for copy in own_copies(s):
@@ -272,15 +272,11 @@
             pass_on(s, go, partner, [along(s, partner, 1)])
             pass_on(s, go, mate, [over(s, mate)])
 
-        @pl.when(is_gate & odd_of(s))
+        @pl.when(is_gate)
         def _():
             pass_on(s, go, partner, [across(s, partner)])
 
     def helped_second(s, go):
-        @pl.when(is_gate & even_of(s))
-        def _():
-            pass_on(s, go, far_gate, [over(s, far_gate)])
-
         @pl.when(is_gate)
         def _():
             pass_on(s, go, far_corner, [over(s, far_corner)])
@@ -320,18 +316,11 @@
             await_block(s, far(k, other))
 
     def await_helped(s):
-        @pl.when(is_gate & even_of(s))
-        def _():
-            await_block(s, partner)
-
-        @pl.when(is_gate & odd_of(s))
+        await_block(s, near(1, other))
+
+        @pl.when(is_gate)
         def _():
             await_block(s, far_gate)
-
-        await_block(s, near(1, other))
-
-        @pl.when(is_gate)
-        def _():
             await_block(s, mate)
             for k in range(half):
                 await_block(s, far(k, other))
@@ -425,8 +414,20 @@
 
     for j in range(1, n_row):
         id_row_copy(j).start()
+    def open_sends(ch):
+        if ch < chunks - 1:
+            send_all(ch)
+        else:
+            for copy in other_copies(ch):
+                copy.start()
+
+            @pl.when(jnp.logical_not(is_gate))
+            def _():
+                for copy in near_copies(ch):
+                    copy.start()
+
     for ch in range(chunks):
-        send_all(ch)
+        open_sends(ch)
 
     for s in range(LEAD1):
         first_relay(jnp.int32(s), True)
@@ -511,6 +512,12 @@
         def _():
             for s in range(LEAD1, chunks):
                 first_relay(jnp.int32(s), True)
+
+            @pl.when(is_gate)
+            def _():
+                for copy in near_copies(chunks - 1):
+                    copy.start()
+
             weight_copy(0).wait()
             for l in range(layers):
                 gain_copy(l).wait()

time: 95 us -> 93.8 us (0.987)
  Pallas kernels: 94.1 us -> 92.9 us
    pallas_call x1, Pallas kernels: 94.1 us -> 92.9 us  [shards(): pl.pallas_call(functools.partial(kernel, sizes), out_shape=jax.ShapeDtype...]
where the time goes in v6:
time: 93.8 us; the launch traced here: 93.6 us
  Pallas kernels  92.9 us (99%)
    pallas_call x1, Pallas kernels, shards(): pl.pallas_call(functools.partial(kernel, sizes), out_shape=jax.ShapeDtype...  92.9 us

profile of v6, /device:TPU:1, one launch (start us, length us, event | category | flops | bytes accessed | tf_op | source)
XLA Modules:
  0.0 93.6 jit_solution(3397622992967674070)
XLA Ops:
  0.0 92.9 %shard_map.55 = bf16[256,512]{1,0:T(8,128)(2,1)S(1)} custom-call(bf16[32,4096]{1,0:T(8,128)(2,1)} %rows_hbm.1, s32[1,32]{1,0:T(1,128)} %bitcast.1, bf16[8,4096]{1,0:T(8,128)(2,1)} %embed_hbm.1, f32[4,4096]{1,0:T(4,128)} %gain_hbm.1, bf16[4,4096,512]{2,1,0:T(8,128)(2,1)} %weight_ref.1), custom_call_target="tpu_custom_call" | custom-call | tf_op jit(solution)/shard_map/pallas_call | solution.py:773
  92.9 0.7 copy.7

commit v7 on v6

--- a/solution.py
+++ b/solution.py
@@ -601,10 +601,6 @@
                 row_copy(ch, j).start()
 
     def after(s, l, ch):
-        @pl.when((l == layers - 1) & (ch >= 2))
-        def _():
-            place(ch - 2)
-
         @pl.when(s == chunks)
         def _():
             pass_ids()
@@ -644,11 +640,21 @@
     near_cols = pl.ds(pl.multiple_of(near_base, width // 2), width // 2)
     far_cols = pl.ds(pl.multiple_of(far_base, width // 2), width // 2)
 
+    def slot_lines(ch):
+        return pl.ds(pl.multiple_of((ch % 2) * m, m), m)
+
+    def own_result(s):
+        l = s // chunks
+        ch = s % chunks
+        update = jnp.dot(active[slot_lines(ch), :], weight[l], preferred_element_type=F32)
+        finish(s, l, ch, (hidden[s, me_c].astype(F32) + update).astype(BF16))
+
     def activate(s, l, begin, inverse):
+        lines = slot_lines(s % chunks)
         for q in range(n_col // 2):
             c = begin * (n_col // 2) + q
             cols = columns(c)
-            active[:m, cols] = silu(hidden[s, c].astype(F32) * inverse * gain[l, :, cols])
+            active[lines, cols] = silu(hidden[s, c].astype(F32) * inverse * gain[l, :, cols])
 
     def helped_step(s, carry):
         l = s // chunks
@@ -681,18 +687,20 @@
             scale_copy(s).start()
             activate(s, l, 1 - side, inverse)
             theirs = helped[l - first_helped].reshape(width // 2, part)
-            part_out[ch] = jnp.dot(active[:m, far_cols], theirs, preferred_element_type=F32).astype(BF16)
+            part_out[ch] = jnp.dot(active[slot_lines(ch), far_cols], theirs, preferred_element_type=F32).astype(BF16)
             part_copy(s).start()
             activate(s, l, side, inverse)
-            update = jnp.dot(active[:m, :], weight[l], preferred_element_type=F32)
-            finish(s, l, ch, (hidden[s, me_c].astype(F32) + update).astype(BF16))
+
+            @pl.when(s > bound)
+            def _():
+                own_result(s - 1)
 
         @pl.when(jnp.logical_not(is_gate))
         def _():
             scale_copy(s).wait_recv()
             inverse = jnp.sum(jnp.where(square, scale_in[s - bound, 0:1, 0:m], 0.0), axis=1, keepdims=True)
             activate(s, l, side, inverse)
-            update = jnp.dot(active[:m, near_cols], weight[l, near_cols, :], preferred_element_type=F32)
+            update = jnp.dot(active[slot_lines(ch), near_cols], weight[l, near_cols, :], preferred_element_type=F32)
             part_copy(s).wait_recv()
             update = update + part_in[s - bound].astype(F32)
             finish(s, l, ch, (hidden[s, me_c].astype(F32) + update).astype(BF16))
@@ -707,6 +715,11 @@
     lax.fori_loop(chunks, bound, step, 0)
     if assisted:
         lax.fori_loop(bound, steps, helped_step, 0)
+
+        @pl.when(is_gate)
+        def _():
+            own_result(jnp.int32(steps - 1))
+
     for ch in range(chunks):
         first_relay(jnp.int32(steps - chunks + ch), False)
         second_relay(jnp.int32(steps - chunks + ch), False)
@@ -724,8 +737,8 @@
     for ch in range(chunks - 1):
         for j in range(1, n_row):
             row_copy(ch, j).wait_send()
-    place(chunks - 2)
-    place(chunks - 1)
+    for ch in range(chunks):
+        place(ch)
     for j in range(1, n_row):
         row_copy(chunks - 1, j).wait_send()
 

time: 93.8 us -> 93 us (level)
  no operation moved by 1% of the time
where the time goes in v7:
time: 93 us; the launch traced here: 92.9 us
  Pallas kernels  92.2 us (99%)
    pallas_call x1, Pallas kernels, shards(): pl.pallas_call(functools.partial(kernel, sizes), out_shape=jax.ShapeDtype...  92.2 us

profile of v7, /device:TPU:1, one launch (start us, length us, event | category | flops | bytes accessed | tf_op | source)
XLA Modules:
  0.0 92.9 jit_solution(7173934185990754866)
XLA Ops:
  0.0 92.2 %shard_map.55 = bf16[256,512]{1,0:T(8,128)(2,1)S(1)} custom-call(bf16[32,4096]{1,0:T(8,128)(2,1)} %rows_hbm.1, s32[1,32]{1,0:T(1,128)} %bitcast.1, bf16[8,4096]{1,0:T(8,128)(2,1)} %embed_hbm.1, f32[4,4096]{1,0:T(4,128)} %gain_hbm.1, bf16[4,4096,512]{2,1,0:T(8,128)(2,1)} %weight_ref.1), custom_call_target="tpu_custom_call" | custom-call | tf_op jit(solution)/shard_map/pallas_call | solution.py:786
  92.2 0.7 copy.7
